TPU v7x, 32 devices: a whole 2x2x4 slice. The times are simulated.
32 devices in a mesh: row: 4 (over z), col: 8 (over y, x, core).
Axes of the slice: x: 2, y: 2, z: 4, core: 2. Of those that a mesh axis runs over, the one named last changes fastest.
Arguments:
- node_feats: bfloat16 [4096, 512], P(('row', 'col')), may hold values from -80 to 80
- block_mask: int32 [32, 32], replicated, may hold values from 0 to 1, as said below
- w_qkv: bfloat16 [2, 512, 1536], replicated, may hold values from -0.25 to 0.25
- w_out: bfloat16 [2, 512, 512], replicated, may hold values from -0.79296875 to 0.79296875
- w_up: bfloat16 [2, 512, 1024], replicated, may hold values from -0.25 to 0.25
- w_down: bfloat16 [2, 1024, 512], replicated, may hold values from -0.1875 to 0.1875
- ln_gain: float32 [2, 2, 512], replicated, may hold values from 0.1 to 1.9
- ln_bias: float32 [2, 2, 512], replicated, may hold values from -3 to 3
Outputs:
- nodes_out: bfloat16 [4096, 512], P(('row', 'col'))
Inputs may be any that keep to these rules, and one draw needn't show every extreme that they name: `block_mask`: A symmetric 0/1 table over the 32 node blocks; every block is linked with itself.
All inputs are finite; a program needn't handle non-finite values.
Results may differ from a plain program's by a relative error of at most 0.022.
Values may be sent and summed in bfloat16 or wider, within the bound.
A program may use at most 128 MiB of HBM per device.

v0:
```python
import jax
import jax.numpy as jnp
from jax import lax
from jax.sharding import PartitionSpec as P

HEADS = 8
BLOCK = 128
LAYERS = 2


def combined_all(x, axis, combine):
    everything = jax.tree.map(
        lambda part, kind: lax.all_gather(part.astype(kind), axis),
        x,
        (jnp.bfloat16, jnp.bfloat16, jnp.bfloat16),
    )

    def take(k):
        return jax.tree.map(lambda part, own: part[k].astype(own.dtype), everything, x)

    return lax.fori_loop(
        1, lax.axis_size(axis), lambda k, so_far: combine(so_far, take(k)), take(0)
    )


def layer_norm(values, gain, bias):
    center = values - jnp.mean(values, axis=-1, keepdims=True)
    spread = jnp.mean(center * center, axis=-1, keepdims=True)
    return center * lax.rsqrt(spread + 1e-05) * gain + bias


def per_head(summed, factor):
    count = summed.shape[0]
    return (summed.reshape(count, factor.shape[1], -1) * factor[:, :, None]).reshape(summed.shape)


def combine(first, second):
    sum_a, peak_a, mass_a = first
    sum_b, peak_b, mass_b = second
    peak = jnp.maximum(peak_a, peak_b)
    scale_a = jnp.exp(peak_a - peak)
    scale_b = jnp.exp(peak_b - peak)
    return (
        per_head(sum_a, scale_a) + per_head(sum_b, scale_b),
        peak,
        mass_a * scale_a + mass_b * scale_b,
    )


def partial_attention(queries, keys, values, sub_mask, heads):
    qrows, width = queries.shape
    head_dim = width // heads
    qblock = min(512, qrows)
    nblocks = qrows // qblock
    qsplit = queries.reshape(nblocks, qblock, heads, head_dim)
    ksplit = keys.reshape(-1, heads, head_dim)
    vsplit = values.reshape(-1, heads, head_dim)
    mask_rows = sub_mask.reshape(nblocks, qblock // BLOCK, -1)

    def one_block(item):
        qpart, mpart = item
        scores = jnp.einsum("qhd,khd->hqk", qpart, ksplit, preferred_element_type=jnp.float32) * (
            1.0 / head_dim**0.5
        )
        allowed = (jnp.repeat(jnp.repeat(mpart, BLOCK, axis=0), BLOCK, axis=1) > 0)[None]
        peak = jnp.max(jnp.where(allowed, scores, -1e30), axis=-1, keepdims=True)
        weights = jnp.where(allowed, jnp.exp(scores - peak), 0.0)
        mass = jnp.sum(weights, axis=-1)
        summed = jnp.einsum(
            "hqk,khd->qhd", weights.astype(jnp.bfloat16), vsplit, preferred_element_type=jnp.float32
        )
        return (summed.reshape(qblock, width), peak[:, :, 0].T, mass.T)

    summed, peak, mass = lax.map(one_block, (qsplit, mask_rows))
    return (summed.reshape(qrows, width), peak.reshape(qrows, heads), mass.reshape(qrows, heads))


def per_device(node_feats, block_mask, w_qkv, w_out, w_up, w_down, ln_gain, ln_bias):
    rows, width = node_feats.shape
    heads = HEADS
    n_col = lax.axis_size("col")
    n_row = lax.axis_size("row")
    row_index = lax.axis_index("row")
    col_index = lax.axis_index("col")
    blk_dev = rows // BLOCK
    group_ids = row_index * (n_col * blk_dev) + jnp.arange(n_col * blk_dev, dtype=jnp.int32)
    column_ids = (
        (jnp.arange(n_row, dtype=jnp.int32)[:, None] * n_col + col_index) * blk_dev
        + jnp.arange(blk_dev, dtype=jnp.int32)[None, :]
    ).reshape(-1)
    query_ids, key_ids, own_start = (column_ids, group_ids, row_index * rows)
    sub_mask = jnp.take(jnp.take(block_mask, query_ids, axis=0), key_ids, axis=1)
    x = node_feats
    for layer in range(LAYERS):
        weights = w_qkv[layer]
        qkv = jnp.dot(x, weights, preferred_element_type=jnp.float32).astype(jnp.bfloat16)
        own_q = qkv[:, :width]
        pair = (qkv[:, width : 2 * width], qkv[:, 2 * width :])
        keys, values = (
            lax.all_gather(pair[0], "col", axis=0, tiled=True),
            lax.all_gather(pair[1], "col", axis=0, tiled=True),
        )
        queries = lax.all_gather(own_q, "row", axis=0, tiled=True)
        summed, peak, mass = partial_attention(queries, keys, values, sub_mask, heads)
        summed, peak, mass = combined_all((summed, peak, mass), "row", combine)
        summed = lax.dynamic_slice_in_dim(summed, own_start, rows, 0)
        mass = lax.dynamic_slice_in_dim(mass, own_start, rows, 0)
        attn = per_head(summed, 1.0 / mass).astype(jnp.bfloat16)
        mixed = jnp.dot(attn, w_out[layer], preferred_element_type=jnp.float32)
        hidden = layer_norm(
            x.astype(jnp.float32) + mixed, ln_gain[layer, 0], ln_bias[layer, 0]
        ).astype(jnp.bfloat16)
        up = jax.nn.gelu(jnp.dot(hidden, w_up[layer], preferred_element_type=jnp.float32)).astype(
            jnp.bfloat16
        )
        down = jnp.dot(up, w_down[layer], preferred_element_type=jnp.float32)
        x = layer_norm(
            hidden.astype(jnp.float32) + down, ln_gain[layer, 1], ln_bias[layer, 1]
        ).astype(jnp.bfloat16)
    return x


def solution(mesh):
    placed = (P(("row", "col"), None), P(), P(), P(), P(), P(), P(), P())
    return jax.shard_map(
        per_device, mesh=mesh, in_specs=placed, out_specs=P(("row", "col"), None), check_vma=False
    )
```

profile of v0, /device:TPU:0, one launch (start us, length us, event | category | flops | bytes accessed | tf_op | source)
XLA Modules:
  0.0 255.1 jit_solution(7514067950112595281)
XLA Ops:
  6.5 1.9 convolution_convert_fusion.1
  11.5 1.6 broadcast_in_dim.118
  13.4 17.4 %all_gather.43 = bf16[512,512]{1,0:T(8,128)(2,1)S(1)} all-gather(bf16[128,512]{1,0:T(8,128)(2,1)S(1)} %get-tuple-element.465), channel_id=1, replica_groups=mesh['row'=4,'col'=8] {'row'}, dimensions={0}, use_global_device_ids=true | all-gather | bytes 655360 | tf_op jit(solution)/shard_map/all_gather | solution.py:103
  31.0 4.4 %all-gather.13.cloned.1.call-done = bf16[1024,512]{1,0:T(8,128)(2,1)} async-done(((bf16[128,512]{1,0:T(8,128)(2,1)}), bf16[1024,512]{1,0:T(8,128)(2,1)}) %all-gather.13.cloned.1.call-update) | async-done | bytes 1048592 | tf_op jit(solution)/shard_map/all_gather | solution.py:100
  35.4 1.5 copy.33
  36.9 7.4 %select_reduce_fusion.1 = (f32[8,512]{1,0:T(8,128)S(1)}, f32[8,512,1024]{2,1,0:T(8,128)}) fusion(pred[512,1024]{1,0:T(8,128)(4,1)S(1)} %bitcast.172, bf16[512,8,64]{0,2,1:T(8,128)(2,1)S(1)} %bitcast.180, bf16[1024,8,64]{0,2,1:T(8,128)(2,1)S(1)} %bitcast.178), kind=kOutput, calls=%fused_computation.25 | convolution fusion | flops 549449728 | bytes 18890752 | tf_op jit(solution)/shard_map/while/body/eval_jaxpr/qhd,khd->hqk/dot_general | solution.py:62
  44.3 16.4 %all-gather.11.cloned.1.call-done = bf16[1024,512]{1,0:T(8,128)(2,1)} async-done(((bf16[128,512]{1,0:T(8,128)(2,1)}), bf16[1024,512]{1,0:T(8,128)(2,1)}) %all-gather.11.cloned.1.call-update) | async-done | bytes 1048592 | tf_op jit(solution)/shard_map/all_gather | solution.py:101
  60.7 1.5 copy.29
  62.2 7.6 %fusion.20 = bf16[8,64,512]{2,1,0:T(8,128)(2,1)S(1)} fusion(bf16[1024,8,64]{0,2,1:T(8,128)(2,1)S(1)} %bitcast.183, f32[8,512,1024]{2,1,0:T(8,128)} %get-tuple-element.476, f32[8,512]{1,0:T(8,128)S(1)} %get-tuple-element.475, pred[512,1024]{1,0:T(8,128)(4,1)S(1)} %bitcast.173), kind=kOutput, calls=%fused_computation.41 | convolution fusion | flops 553910272 | bytes 18890752 | tf_op jit(solution)/shard_map/while/body/eval_jaxpr/hqk,khd->qhd/dot_general | solution.py:69
  70.9 8.2 %fusion.6 = bf16[8,512]{1,0:T(8,128)(2,1)S(1)} fusion(f32[8,512,1024]{2,1,0:T(8,128)} %get-tuple-element.476, f32[8,512]{1,0:T(8,128)S(1)} %get-tuple-element.475, pred[512,1024]{1,0:T(8,128)(4,1)S(1)} %bitcast.174), kind=kLoop, calls=%fused_computation.26 | loop fusion | flops 16773120 | bytes 17326080 | tf_op jit(solution)/shard_map/while/body/eval_jaxpr/reduce_sum | solution.py:68
  79.2 13.9 %all-gather.1 = bf16[2048,8]{0,1:T(8,128)(2,1)S(1)} all-gather(bf16[512,8]{0,1:T(8,128)(2,1)S(1)} %bitcast.193), channel_id=3, replica_groups=mesh['row'=4,'col'=8] {'row'}, dimensions={0}, use_global_device_ids=true | all-gather | bytes 40960 | tf_op jit(solution)/shard_map/all_gather | solution.py:13
  93.1 13.7 %all-gather = bf16[2048,8]{0,1:T(8,128)(2,1)S(1)} all-gather(bf16[512,8]{0,1:T(8,128)(2,1)S(1)} %convert_bitcast_fusion.3), channel_id=2, replica_groups=mesh['row'=4,'col'=8] {'row'}, dimensions={0}, use_global_device_ids=true | all-gather | bytes 40960 | tf_op jit(solution)/shard_map/all_gather | solution.py:13
  106.8 10.9 %all-gather.15.cloned.1.call-done = bf16[4,512,512]{2,1,0:T(8,128)(2,1)} async-done(((bf16[1,512,512]{2,1,0:T(8,128)(2,1)}), bf16[4,512,512]{2,1,0:T(8,128)(2,1)}) %all-gather.15.cloned.1.call-update) | async-done | bytes 2097168 | tf_op jit(solution)/shard_map/all_gather | solution.py:13
  119.2 5.7 %while.24 = (s32[]{:T(128)}, f32[512,512]{0,1:T(8,128)S(1)}, f32[512,8]{0,1:T(8,128)S(1)}, f32[512,8]{0,1:T(8,128)S(1)}, bf16[4,512,8]{1,2,0:T(8,128)(2,1)S(1)},...) while((s32[]{:T(128)}, f32[512,512]{0,1:T(8,128)S(1)}, ...), condition=%wide.region_3.4_spmd, body=%wide.region_2.3_spmd.sunk | while | flops 1081349 | bytes 4866191 | solution.py:21
  125.0 1.4 fusion.117
  126.6 2.2 fusion.118
  129.0 1.8 convolution_convert_fusion
  132.3 15.7 %all_gather.49 = bf16[512,512]{1,0:T(8,128)(2,1)S(1)} all-gather(bf16[128,512]{1,0:T(8,128)(2,1)S(1)} %get-tuple-element.462), channel_id=1, replica_groups=mesh['row'=4,'col'=8] {'row'}, dimensions={0}, use_global_device_ids=true | all-gather | bytes 655360 | tf_op jit(solution)/shard_map/all_gather | solution.py:103
  148.2 5.7 %all-gather.19.cloned.1.call-done = bf16[1024,512]{1,0:T(8,128)(2,1)} async-done(((bf16[128,512]{1,0:T(8,128)(2,1)}), bf16[1024,512]{1,0:T(8,128)(2,1)}) %all-gather.19.cloned.1.call-update) | async-done | bytes 1048592 | tf_op jit(solution)/shard_map/all_gather | solution.py:100
  154.0 1.5 copy.39
  155.5 7.4 %select_reduce_fusion = (f32[8,512]{1,0:T(8,128)S(1)}, f32[8,512,1024]{2,1,0:T(8,128)}) fusion(pred[512,1024]{1,0:T(8,128)(4,1)S(1)} %bitcast.175, bf16[512,8,64]{0,2,1:T(8,128)(2,1)S(1)} %bitcast.181, bf16[1024,8,64]{0,2,1:T(8,128)(2,1)S(1)} %bitcast.179), kind=kOutput, calls=%fused_computation.23 | convolution fusion | flops 549449728 | bytes 18890752 | tf_op jit(solution)/shard_map/while/body/eval_jaxpr/qhd,khd->hqk/dot_general | solution.py:62
  162.9 16.2 %all-gather.17.cloned.1.call-done = bf16[1024,512]{1,0:T(8,128)(2,1)} async-done(((bf16[128,512]{1,0:T(8,128)(2,1)}), bf16[1024,512]{1,0:T(8,128)(2,1)}) %all-gather.17.cloned.1.call-update) | async-done | bytes 1048592 | tf_op jit(solution)/shard_map/all_gather | solution.py:101
  179.1 1.5 copy.37
  180.6 7.6 %fusion.23 = bf16[8,64,512]{2,1,0:T(8,128)(2,1)S(1)} fusion(bf16[1024,8,64]{0,2,1:T(8,128)(2,1)S(1)} %bitcast.184, f32[8,512,1024]{2,1,0:T(8,128)} %get-tuple-element.482, f32[8,512]{1,0:T(8,128)S(1)} %get-tuple-element.481, pred[512,1024]{1,0:T(8,128)(4,1)S(1)} %bitcast.176), kind=kOutput, calls=%fused_computation.42 | convolution fusion | flops 553910272 | bytes 18890752 | tf_op jit(solution)/shard_map/while/body/eval_jaxpr/hqk,khd->qhd/dot_general | solution.py:69
  189.2 8.2 %fusion.8 = bf16[8,512]{1,0:T(8,128)(2,1)S(1)} fusion(f32[8,512,1024]{2,1,0:T(8,128)} %get-tuple-element.482, f32[8,512]{1,0:T(8,128)S(1)} %get-tuple-element.481, pred[512,1024]{1,0:T(8,128)(4,1)S(1)} %bitcast.177), kind=kLoop, calls=%fused_computation.28 | loop fusion | flops 16773120 | bytes 17326080 | tf_op jit(solution)/shard_map/while/body/eval_jaxpr/reduce_sum | solution.py:68
  197.5 13.7 %all-gather.3 = bf16[2048,8]{0,1:T(8,128)(2,1)S(1)} all-gather(bf16[512,8]{0,1:T(8,128)(2,1)S(1)} %bitcast.192), channel_id=5, replica_groups=mesh['row'=4,'col'=8] {'row'}, dimensions={0}, use_global_device_ids=true | all-gather | bytes 40960 | tf_op jit(solution)/shard_map/all_gather | solution.py:13
  211.2 13.8 %all-gather.2 = bf16[2048,8]{0,1:T(8,128)(2,1)S(1)} all-gather(bf16[512,8]{0,1:T(8,128)(2,1)S(1)} %convert_bitcast_fusion.1), channel_id=4, replica_groups=mesh['row'=4,'col'=8] {'row'}, dimensions={0}, use_global_device_ids=true | all-gather | bytes 40960 | tf_op jit(solution)/shard_map/all_gather | solution.py:13
  225.0 11.1 %all-gather.21.cloned.1.call-done = bf16[4,512,512]{2,1,0:T(8,128)(2,1)} async-done(((bf16[1,512,512]{2,1,0:T(8,128)(2,1)}), bf16[4,512,512]{2,1,0:T(8,128)(2,1)}) %all-gather.21.cloned.1.call-update) | async-done | bytes 2097168 | tf_op jit(solution)/shard_map/all_gather | solution.py:13
  236.1 1.2 fusion.64
  237.6 5.7 %while.25 = (s32[]{:T(128)}, f32[512,512]{0,1:T(8,128)S(1)}, f32[512,8]{0,1:T(8,128)S(1)}, f32[512,8]{0,1:T(8,128)S(1)}, bf16[4,512,8]{1,2,0:T(8,128)(2,1)S(1)},...) while((s32[]{:T(128)}, f32[512,512]{0,1:T(8,128)S(1)}, ...), condition=%wide.region_11.12_spmd, body=%wide.region_10.11_spmd.sunk | while | flops 1081349 | bytes 4866191 | solution.py:21
  243.4 1.4 fusion.121
  245.0 2.2 fusion.122
  (94 shorter events, 21.9 us)
Async XLA Ops:
  6.5 3.5 %copy-start = (s32[32,32]{1,0:T(8,128)S(1)}, s32[32,32]{1,0:T(8,128)}, u32[]{:S(2)}) copy-start(s32[32,32]{1,0:T(8,128)} %param.13) | copy-start | bytes 12292
  6.5 28.9 %all-gather.13.cloned.1.call-start = ((), (), s32[]{:S(2)}) async-start(), calls=%async_computation.1 | async-start | bytes 1179648 | tf_op jit(solution)/shard_map/all_gather | solution.py:100
  9.2 51.5 %all-gather.11.cloned.1.call-start = ((), (), s32[]{:S(2)}) async-start(), calls=%async_computation | async-start | bytes 1179648 | tf_op jit(solution)/shard_map/all_gather | solution.py:101
  9.9 107.8 %all-gather.15.cloned.1.call-start = ((), (), s32[]{:S(2)}) async-start(), calls=%async_computation.2 | async-start | bytes 2621440 | tf_op jit(solution)/shard_map/all_gather | solution.py:13
  44.3 26.6 %copy-start.3 = (f32[2,2,512]{2,1,0:T(2,128)S(1)}, f32[2,2,512]{2,1,0:T(2,128)}, u32[]{:S(2)}) copy-start(f32[2,2,512]{2,1,0:T(2,128)} %param.18) | copy-start | bytes 24580
  44.3 26.6 %copy-start.4 = (f32[2,2,512]{2,1,0:T(2,128)S(1)}, f32[2,2,512]{2,1,0:T(2,128)}, u32[]{:S(2)}) copy-start(f32[2,2,512]{2,1,0:T(2,128)} %param.19) | copy-start | bytes 24580
  70.8 83.1 %all-gather.19.cloned.1.call-start = ((), (), s32[]{:S(2)}) async-start(), calls=%async_computation.4 | async-start | bytes 1179648 | tf_op jit(solution)/shard_map/all_gather | solution.py:100
  79.2 45.8 %copy-start.2 = (bf16[128,512]{1,0:T(8,128)(2,1)S(1)}, bf16[128,512]{1,0:T(8,128)(2,1)}, u32[]{:S(2)}) copy-start(bf16[128,512]{1,0:T(8,128)(2,1)} %param.12) | copy-start | bytes 393220
  131.6 47.5 %all-gather.17.cloned.1.call-start = ((), (), s32[]{:S(2)}) async-start(), calls=%async_computation.3 | async-start | bytes 1179648 | tf_op jit(solution)/shard_map/all_gather | solution.py:101
  132.2 103.9 %all-gather.21.cloned.1.call-start = ((), (), s32[]{:S(2)}) async-start(), calls=%async_computation.5 | async-start | bytes 2621440 | tf_op jit(solution)/shard_map/all_gather | solution.py:13
  236.1 12.1 %copy-start.1 = (s32[32,32]{1,0:T(8,128)S(1)}, s32[32,32]{1,0:T(8,128)}, u32[]{:S(2)}) copy-start(s32[32,32]{1,0:T(8,128)} %param.13) | copy-start | bytes 12292
Sparse Core Ops, SparseCore 0:
  9.3 26.0 all-gather.12
  37.3 23.3 all-gather.10
  71.0 46.6 all-gather.14
  131.8 22.1 all-gather.18
  155.7 23.3 all-gather.16
  189.4 46.6 all-gather.20
where the time goes:
time: 256 us; the launch traced here: 255 us
  blocking collectives  88.2 us (34%)
  waiting for transfers between devices  66.1 us (26%)
  matrix products  41 us (16%)
  other arithmetic  24.1 us (9%)
  local copies, waits for them, and re-layouts  21.5 us (8%)
  between operations  13.8 us (5%)
    all_gather x4, blocking collectives, combined_all(): lax.all_gather(part.astype(kind), axis)  55.1 us
    all_gather x2, blocking collectives, per_device(): queries = lax.all_gather(own_q, 'row', axis=0, tiled=True)  33.1 us
    all_gather x2, waiting for transfers between devices, per_device(): lax.all_gather(pair[1], 'col', axis=0, tiled=True)  32.6 us
    all_gather x2, waiting for transfers between devices, combined_all(): lax.all_gather(part.astype(kind), axis)  22 us
    reduce_sum x2, other arithmetic, one_block(): mass = jnp.sum(weights, axis=-1)  16.4 us
    dot_general x2, matrix products, one_block(): jnp.einsum('hqk,khd->qhd', weights.astype(jnp.bfloat16), vsplit, preferre...  15.2 us
    dot_general x2, matrix products, one_block(): jnp.einsum('qhd,khd->hqk', qpart, ksplit, preferred_element_type=jnp.floa...  14.8 us
    all_gather x2, waiting for transfers between devices, per_device(): lax.all_gather(pair[0], 'col', axis=0, tiled=True)  10.1 us
  transfers between devices with their start and end apart: 6, of which 6 were waited for; matrix products, arithmetic and copies ran while one was open for 15% of the time, Pallas kernels for 0%

commit v1 on v0

--- a/solution.py
+++ b/solution.py
@@ -6,6 +6,29 @@
 HEADS = 8
 BLOCK = 128
 LAYERS = 2
+
+
+def laid_out(pieces, dim):
+    shape = list(pieces.shape[1:])
+    shape[dim] *= pieces.shape[0]
+    return jnp.moveaxis(pieces, 0, dim).reshape(shape)
+
+
+def grow_blocks(x, axis):
+    size, index = (lax.axis_size(axis), lax.axis_index(axis))
+    blocks, distance = (x[None], 1)
+    while distance < size:
+        received = lax.ppermute(blocks, axis, [(i, i ^ distance) for i in range(size)])
+        low = index & distance == 0
+        blocks = jnp.concatenate(
+            [jnp.where(low, blocks, received), jnp.where(low, received, blocks)]
+        )
+        distance *= 2
+    return blocks
+
+
+def collect(x, axis, dim):
+    return laid_out(grow_blocks(x, axis), dim)
 
 
 def combined_all(x, axis, combine):
@@ -97,7 +120,7 @@
         own_q = qkv[:, :width]
         pair = (qkv[:, width : 2 * width], qkv[:, 2 * width :])
         keys, values = (
-            lax.all_gather(pair[0], "col", axis=0, tiled=True),
+            collect(pair[0], "col", 0),
             lax.all_gather(pair[1], "col", axis=0, tiled=True),
         )
         queries = lax.all_gather(own_q, "row", axis=0, tiled=True)

time: 256 us -> 233 us (0.910)
  waiting for transfers between devices: 66.1 us -> 34 us
  starting transfers between devices: 0.2 us -> 8.4 us
  other arithmetic: 24.1 us -> 27 us
    all_gather x2, waiting for transfers between devices: 32.6 us -> 0.01 us  [per_device(): lax.all_gather(pair[1], 'col', axis=0, tiled=True)]
    ppermute x0 -> x6, waiting for transfers between devices: none -> 14.4 us  [grow_blocks(): lax.ppermute(blocks, axis, [(i, i ^ distance) for i in range(size)])]
    all_gather x2 -> x0, waiting for transfers between devices: 10.1 us -> none  [per_device(): lax.all_gather(pair[0], 'col', axis=0, tiled=True)]
    ppermute x0 -> x6, starting transfers between devices: none -> 8.27 us  [grow_blocks(): lax.ppermute(blocks, axis, [(i, i ^ distance) for i in range(size)])]
    all_gather x2 -> x0, local copies, waits for them, and re-layouts: 2.96 us -> none  [per_device(): lax.all_gather(pair[0], 'col', axis=0, tiled=True)]
  transfers between devices with their start and end apart: 6 -> 10, of which waited for: 6 -> 6; matrix products, arithmetic and copies ran while one was open for 15% -> 17% of each run, Pallas kernels for 0% -> 0%
where the time goes in v1:
time: 233 us; the launch traced here: 232 us
  blocking collectives  87.3 us (37%)
  matrix products  40.9 us (18%)
  waiting for transfers between devices  34 us (15%)
  other arithmetic  27 us (12%)
  local copies, waits for them, and re-layouts  21 us (9%)
  between operations  13.6 us (6%)
  starting transfers between devices  8.4 us (4%)
    all_gather x4, blocking collectives, combined_all(): lax.all_gather(part.astype(kind), axis)  55.9 us
    all_gather x2, blocking collectives, per_device(): queries = lax.all_gather(own_q, 'row', axis=0, tiled=True)  31.3 us
    all_gather x2, waiting for transfers between devices, combined_all(): lax.all_gather(part.astype(kind), axis)  19.6 us
    reduce_sum x2, other arithmetic, one_block(): mass = jnp.sum(weights, axis=-1)  16.6 us
    dot_general x2, matrix products, one_block(): jnp.einsum('hqk,khd->qhd', weights.astype(jnp.bfloat16), vsplit, preferre...  15.2 us
    dot_general x2, matrix products, one_block(): jnp.einsum('qhd,khd->hqk', qpart, ksplit, preferred_element_type=jnp.floa...  14.7 us
    ppermute x6, waiting for transfers between devices, grow_blocks(): lax.ppermute(blocks, axis, [(i, i ^ distance) for i in range(size)])  14.4 us
    ppermute x6, starting transfers between devices, grow_blocks(): lax.ppermute(blocks, axis, [(i, i ^ distance) for i in range(size)])  8.27 us
  transfers between devices with their start and end apart: 10, of which 6 were waited for; matrix products, arithmetic and copies ran while one was open for 17% of the time, Pallas kernels for 0%

profile of v1, /device:TPU:0, one launch (start us, length us, event | category | flops | bytes accessed | tf_op | source)
XLA Modules:
  0.0 232.3 jit_solution(8189530725284435670)
XLA Ops:
  6.5 1.9 convolution_convert_fusion.1
  10.6 2.9 %collective-permute-start.1 = (bf16[2,128,512]{2,1,0:T(8,128)(2,1)S(1)}, bf16[2,128,512]{2,1,0:T(8,128)(2,1)S(1)}, u32[]{:S(2)}, u32[]{:S(2)}) collective-permute-start(bf16[2,128,512]{2,1,0:T(8,128)(2,1)S(1)} %pad_maximum_fusion.4), channel_id=1, source_target_pairs={{0,2},{1,3},{2,0},{3,1},{4,6},{5,7},{6,4},{7,5},{8,10},{9,11},{10,... | collective-permute-start | bytes 786440 | tf_op jit(solution)/shard_map/ppermute | solution.py:21
  14.3 5.9 %collective-permute-done.1 = bf16[2,128,512]{2,1,0:T(8,128)(2,1)S(1)} collective-permute-done((bf16[2,128,512]{2,1,0:T(8,128)(2,1)S(1)}, bf16[2,128,512]{2,1,0:T(8,128)(2,1)S(1)}, u32[]{:S(2)}, u32[]{:S(2)}) %collective-permute-start.1) | collective-permute-done | bytes 262176 | tf_op jit(solution)/shard_map/ppermute | solution.py:21
  20.3 1.8 collective-permute-start.2
  22.3 1.6 broadcast_in_dim.124
  24.2 15.2 %all_gather.37 = bf16[512,512]{1,0:T(8,128)(2,1)S(1)} all-gather(bf16[128,512]{1,0:T(8,128)(2,1)S(1)} %get-tuple-element.477), channel_id=1, replica_groups=mesh['row'=4,'col'=8] {'row'}, dimensions={0}, use_global_device_ids=true | all-gather | bytes 655360 | tf_op jit(solution)/shard_map/all_gather | solution.py:126
  42.1 7.4 %select_reduce_fusion.1 = (f32[8,512]{1,0:T(8,128)S(1)}, f32[8,512,1024]{2,1,0:T(8,128)}) fusion(pred[512,1024]{1,0:T(8,128)(4,1)S(1)} %bitcast.186, bf16[512,8,64]{0,2,1:T(8,128)(2,1)S(1)} %bitcast.193, bf16[1024,8,64]{0,2,1:T(8,128)(2,1)S(1)} %reshape_reshape.6), kind=kOutput, calls=%fused_computation.25 | convolution fusion | flops 549449728 | bytes 18890752 | tf_op jit(solution)/shard_map/while/body/eval_jaxpr/qhd,khd->hqk/dot_general | solution.py:85
  49.4 1.5 copy.29
  51.0 7.6 %fusion.20 = bf16[8,64,512]{2,1,0:T(8,128)(2,1)S(1)} fusion(bf16[1024,8,64]{0,2,1:T(8,128)(2,1)S(1)} %bitcast.195, f32[8,512,1024]{2,1,0:T(8,128)} %get-tuple-element.488, f32[8,512]{1,0:T(8,128)S(1)} %get-tuple-element.487, pred[512,1024]{1,0:T(8,128)(4,1)S(1)} %bitcast.187), kind=kOutput, calls=%fused_computation.41 | convolution fusion | flops 553910272 | bytes 18890752 | tf_op jit(solution)/shard_map/while/body/eval_jaxpr/hqk,khd->qhd/dot_general | solution.py:92
  59.7 8.2 %fusion.6 = bf16[8,512]{1,0:T(8,128)(2,1)S(1)} fusion(f32[8,512,1024]{2,1,0:T(8,128)} %get-tuple-element.488, f32[8,512]{1,0:T(8,128)S(1)} %get-tuple-element.487, pred[512,1024]{1,0:T(8,128)(4,1)S(1)} %bitcast.188), kind=kLoop, calls=%fused_computation.26 | loop fusion | flops 16773120 | bytes 17326080 | tf_op jit(solution)/shard_map/while/body/eval_jaxpr/reduce_sum | solution.py:91
  67.9 14.0 %all-gather.1 = bf16[2048,8]{0,1:T(8,128)(2,1)S(1)} all-gather(bf16[512,8]{0,1:T(8,128)(2,1)S(1)} %bitcast.205), channel_id=3, replica_groups=mesh['row'=4,'col'=8] {'row'}, dimensions={0}, use_global_device_ids=true | all-gather | bytes 40960 | tf_op jit(solution)/shard_map/all_gather | solution.py:36
  81.9 14.2 %all-gather = bf16[2048,8]{0,1:T(8,128)(2,1)S(1)} all-gather(bf16[512,8]{0,1:T(8,128)(2,1)S(1)} %convert_bitcast_fusion.3), channel_id=2, replica_groups=mesh['row'=4,'col'=8] {'row'}, dimensions={0}, use_global_device_ids=true | all-gather | bytes 40960 | tf_op jit(solution)/shard_map/all_gather | solution.py:36
  96.1 11.0 %all-gather.11.cloned.1.call-done = bf16[4,512,512]{2,1,0:T(8,128)(2,1)} async-done(((bf16[1,512,512]{2,1,0:T(8,128)(2,1)}), bf16[4,512,512]{2,1,0:T(8,128)(2,1)}) %all-gather.11.cloned.1.call-update) | async-done | bytes 2097168 | tf_op jit(solution)/shard_map/all_gather | solution.py:36
  108.7 5.7 %while.24 = (s32[]{:T(128)}, f32[512,512]{0,1:T(8,128)S(1)}, f32[512,8]{0,1:T(8,128)S(1)}, f32[512,8]{0,1:T(8,128)S(1)}, bf16[4,512,8]{1,2,0:T(8,128)(2,1)S(1)},...) while((s32[]{:T(128)}, f32[512,512]{0,1:T(8,128)S(1)}, ...), condition=%wide.region_3.4_spmd, body=%wide.region_2.3_spmd.sunk | while | flops 1081349 | bytes 4866199 | solution.py:44
  114.5 1.4 fusion.115
  116.0 2.2 fusion.116
  118.5 1.8 convolution_convert_fusion
  121.0 1.3 collective-permute-done.3
  122.4 1.5 collective-permute-start.4
  124.0 6.8 %collective-permute-done.4 = bf16[2,128,512]{2,1,0:T(8,128)(2,1)S(1)} collective-permute-done((bf16[2,128,512]{2,1,0:T(8,128)(2,1)S(1)}, bf16[2,128,512]{2,1,0:T(8,128)(2,1)S(1)}, u32[]{:S(2)}, u32[]{:S(2)}) %collective-permute-start.4) | collective-permute-done | bytes 262176 | tf_op jit(solution)/shard_map/ppermute | solution.py:21
  131.0 1.5 collective-permute-start.5
  132.5 16.2 %all_gather.42 = bf16[512,512]{1,0:T(8,128)(2,1)S(1)} all-gather(bf16[128,512]{1,0:T(8,128)(2,1)S(1)} %get-tuple-element.474), channel_id=1, replica_groups=mesh['row'=4,'col'=8] {'row'}, dimensions={0}, use_global_device_ids=true | all-gather | bytes 655360 | tf_op jit(solution)/shard_map/all_gather | solution.py:126
  151.4 7.4 %select_reduce_fusion = (f32[8,512]{1,0:T(8,128)S(1)}, f32[8,512,1024]{2,1,0:T(8,128)}) fusion(pred[512,1024]{1,0:T(8,128)(4,1)S(1)} %bitcast.189, bf16[512,8,64]{0,2,1:T(8,128)(2,1)S(1)} %bitcast.192, bf16[1024,8,64]{0,2,1:T(8,128)(2,1)S(1)} %reshape_reshape.7), kind=kOutput, calls=%fused_computation.23 | convolution fusion | flops 549449728 | bytes 18890752 | tf_op jit(solution)/shard_map/while/body/eval_jaxpr/qhd,khd->hqk/dot_general | solution.py:85
  158.7 1.5 copy.37
  160.2 7.6 %fusion.23 = bf16[8,64,512]{2,1,0:T(8,128)(2,1)S(1)} fusion(bf16[1024,8,64]{0,2,1:T(8,128)(2,1)S(1)} %bitcast.196, f32[8,512,1024]{2,1,0:T(8,128)} %get-tuple-element.494, f32[8,512]{1,0:T(8,128)S(1)} %get-tuple-element.493, pred[512,1024]{1,0:T(8,128)(4,1)S(1)} %bitcast.190), kind=kOutput, calls=%fused_computation.42 | convolution fusion | flops 553910272 | bytes 18890752 | tf_op jit(solution)/shard_map/while/body/eval_jaxpr/hqk,khd->qhd/dot_general | solution.py:92
  168.9 8.5 %fusion.8 = bf16[8,512]{1,0:T(8,128)(2,1)S(1)} fusion(f32[8,512,1024]{2,1,0:T(8,128)} %get-tuple-element.494, f32[8,512]{1,0:T(8,128)S(1)} %get-tuple-element.493, pred[512,1024]{1,0:T(8,128)(4,1)S(1)} %bitcast.191), kind=kLoop, calls=%fused_computation.28 | loop fusion | flops 16773120 | bytes 17326080 | tf_op jit(solution)/shard_map/while/body/eval_jaxpr/reduce_sum | solution.py:91
  177.3 13.8 %all-gather.3 = bf16[2048,8]{0,1:T(8,128)(2,1)S(1)} all-gather(bf16[512,8]{0,1:T(8,128)(2,1)S(1)} %bitcast.204), channel_id=5, replica_groups=mesh['row'=4,'col'=8] {'row'}, dimensions={0}, use_global_device_ids=true | all-gather | bytes 40960 | tf_op jit(solution)/shard_map/all_gather | solution.py:36
  191.2 13.9 %all-gather.2 = bf16[2048,8]{0,1:T(8,128)(2,1)S(1)} all-gather(bf16[512,8]{0,1:T(8,128)(2,1)S(1)} %convert_bitcast_fusion.1), channel_id=4, replica_groups=mesh['row'=4,'col'=8] {'row'}, dimensions={0}, use_global_device_ids=true | all-gather | bytes 40960 | tf_op jit(solution)/shard_map/all_gather | solution.py:36
  205.1 8.6 %all-gather.15.cloned.1.call-done = bf16[4,512,512]{2,1,0:T(8,128)(2,1)} async-done(((bf16[1,512,512]{2,1,0:T(8,128)(2,1)}), bf16[4,512,512]{2,1,0:T(8,128)(2,1)}) %all-gather.15.cloned.1.call-update) | async-done | bytes 2097168 | tf_op jit(solution)/shard_map/all_gather | solution.py:36
  215.2 5.7 %while.25 = (s32[]{:T(128)}, f32[512,512]{0,1:T(8,128)S(1)}, f32[512,8]{0,1:T(8,128)S(1)}, f32[512,8]{0,1:T(8,128)S(1)}, bf16[4,512,8]{1,2,0:T(8,128)(2,1)S(1)},...) while((s32[]{:T(128)}, f32[512,512]{0,1:T(8,128)S(1)}, ...), condition=%wide.region_11.12_spmd, body=%wide.region_10.11_spmd.sunk | while | flops 1081349 | bytes 4866199 | solution.py:44
  221.0 1.4 fusion.119
  222.6 2.2 fusion.120
  (114 shorter events, 27.7 us)
Async XLA Ops:
  6.5 3.2 %copy-start = (s32[32,32]{1,0:T(8,128)S(1)}, s32[32,32]{1,0:T(8,128)}, u32[]{:S(2)}) copy-start(s32[32,32]{1,0:T(8,128)} %param.13) | copy-start | bytes 12292
  6.5 42.9 %all-gather.9.cloned.1.call-start = ((), (), s32[]{:S(2)}) async-start(), calls=%async_computation | async-start | bytes 1179648 | tf_op jit(solution)/shard_map/all_gather | solution.py:124
  9.1 1.5 collective-permute-start
  9.6 97.5 %all-gather.11.cloned.1.call-start = ((), (), s32[]{:S(2)}) async-start(), calls=%async_computation.1 | async-start | bytes 2621440 | tf_op jit(solution)/shard_map/all_gather | solution.py:36
  10.6 9.5 %collective-permute-start.1 = (bf16[2,128,512]{2,1,0:T(8,128)(2,1)S(1)}, bf16[2,128,512]{2,1,0:T(8,128)(2,1)S(1)}, u32[]{:S(2)}, u32[]{:S(2)}) collective-permute-start(bf16[2,128,512]{2,1,0:T(8,128)(2,1)S(1)} %pad_maximum_fusion.4), channel_id=1, source_target_pairs={{0,2},{1,3},{2,0},{3,1},{4,6},{5,7},{6,4},{7,5},{8,10},{9,11},{10,... | collective-permute-start | bytes 786440 | tf_op jit(solution)/shard_map/ppermute | solution.py:21
  20.3 19.3 %collective-permute-start.2 = (bf16[4,128,512]{2,1,0:T(8,128)(2,1)S(1)}, bf16[4,128,512]{2,1,0:T(8,128)(2,1)}, u32[]{:S(2)}, u32[]{:S(2)}) collective-permute-start(bf16[4,128,512]{2,1,0:T(8,128)(2,1)S(1)} %pad_maximum_fusion.2), channel_id=1, source_target_pairs={{0,4},{1,5},{2,6},{3,7},{4,0},{5,1},{6,2},{7,3},{8,12},{9,13},{10,... | collective-permute-start | bytes 1572872 | tf_op jit(solution)/shard_map/ppermute | solution.py:21
  49.4 10.2 %copy-start.3 = (f32[2,2,512]{2,1,0:T(2,128)S(1)}, f32[2,2,512]{2,1,0:T(2,128)}, u32[]{:S(2)}) copy-start(f32[2,2,512]{2,1,0:T(2,128)} %param.18) | copy-start | bytes 24580
  49.4 10.2 %copy-start.4 = (f32[2,2,512]{2,1,0:T(2,128)S(1)}, f32[2,2,512]{2,1,0:T(2,128)}, u32[]{:S(2)}) copy-start(f32[2,2,512]{2,1,0:T(2,128)} %param.19) | copy-start | bytes 24580
  59.6 99.1 %all-gather.13.cloned.1.call-start = ((), (), s32[]{:S(2)}) async-start(), calls=%async_computation.2 | async-start | bytes 1179648 | tf_op jit(solution)/shard_map/all_gather | solution.py:124
  67.9 46.6 %copy-start.2 = (bf16[128,512]{1,0:T(8,128)(2,1)S(1)}, bf16[128,512]{1,0:T(8,128)(2,1)}, u32[]{:S(2)}) copy-start(bf16[128,512]{1,0:T(8,128)(2,1)} %param.12) | copy-start | bytes 393220
  121.0 1.3 collective-permute-start.3
  122.4 8.4 %collective-permute-start.4 = (bf16[2,128,512]{2,1,0:T(8,128)(2,1)S(1)}, bf16[2,128,512]{2,1,0:T(8,128)(2,1)S(1)}, u32[]{:S(2)}, u32[]{:S(2)}) collective-permute-start(bf16[2,128,512]{2,1,0:T(8,128)(2,1)S(1)} %pad_maximum_fusion.5), channel_id=1, source_target_pairs={{0,2},{1,3},{2,0},{3,1},{4,6},{5,7},{6,4},{7,5},{8,10},{9,11},{10,... | collective-permute-start | bytes 786440 | tf_op jit(solution)/shard_map/ppermute | solution.py:21
  124.0 89.7 %all-gather.15.cloned.1.call-start = ((), (), s32[]{:S(2)}) async-start(), calls=%async_computation.3 | async-start | bytes 2621440 | tf_op jit(solution)/shard_map/all_gather | solution.py:36
  131.0 17.9 %collective-permute-start.5 = (bf16[4,128,512]{2,1,0:T(8,128)(2,1)S(1)}, bf16[4,128,512]{2,1,0:T(8,128)(2,1)}, u32[]{:S(2)}, u32[]{:S(2)}) collective-permute-start(bf16[4,128,512]{2,1,0:T(8,128)(2,1)S(1)} %pad_maximum_fusion.3), channel_id=1, source_target_pairs={{0,4},{1,5},{2,6},{3,7},{4,0},{5,1},{6,2},{7,3},{8,12},{9,13},{10,... | collective-permute-start | bytes 1572872 | tf_op jit(solution)/shard_map/ppermute | solution.py:21
  213.7 12.1 %copy-start.1 = (s32[32,32]{1,0:T(8,128)S(1)}, s32[32,32]{1,0:T(8,128)}, u32[]{:S(2)}) copy-start(s32[32,32]{1,0:T(8,128)} %param.13) | copy-start | bytes 12292
Sparse Core Ops, SparseCore 0:
  9.7 29.1 all-gather.8
  59.7 47.3 all-gather.10
  124.1 24.6 all-gather.12
  169.0 44.6 all-gather.14
